TPU v7x, 512 devices: a 4x2x32 block of a 4x8x32 slice. The times are simulated.
512 devices in a mesh: groups: 2 (over y), aa: 32 (over z), ba: 4 (over x), col: 2 (over core).
Axes of the slice: x: 4, y: 2, z: 32, core: 2. Of those that a mesh axis runs over, the one named last changes fastest.
The devices are a block of a 4x8x32 slice.
Arguments:
- hidden: bfloat16 [256, 128, 8192], P(('groups', 'aa'), None, ('ba', 'col')), parts along dimension 0, may hold values from -6 to 6
- key_value_weight: bfloat16 [2048, 8192], P('aa', ('ba', 'col')), may hold values from -0.125 to 0.125
- adapter_down_weight: bfloat16 [256, 32, 8192], P(('groups', 'aa'), None, ('ba', 'col')), parts along dimension 0, may hold values from -0.0625 to 0.0625
- adapter_up_weight: bfloat16 [256, 16, 2048], P(('groups', 'aa'), None, ('ba', 'col')), parts along dimension 0, may hold values from -1.5 to 1.5
- prompt_block_count: int32 [128], P('groups'), parts along dimension 0, may hold values from 1 to 3, 128 in all
- request_adapter: int32 [128], P('groups'), parts along dimension 0, may hold values from 0 to 127
- adapter_bank_row: int32 [256], P('groups'), parts along dimension 0, may hold values from 0 to 127, each once
Outputs:
- kv_states: bfloat16 [256, 128, 2048], P(('groups', 'aa'), None, ('ba', 'col')), parts along dimension 0
There are 2 independent parts, one for each index of `groups`. A program takes and returns all parts, laid end to end along the dimension named above; an argument that names none is the same for every part. Nothing has to cross between parts.
Inputs may be any that keep to these rules, and one draw needn't show every extreme that they name: prompt_block_count sum to 128; some request has exactly 3 blocks. `adapter_bank_row`: each bank row holds one adapter; bank row s lies on index s // 4 of aa.
All inputs are finite; a program needn't handle non-finite values.
Results may differ from a plain program's by a relative error of at most 0.001.
Values may be sent and summed in bfloat16 or wider, within the bound.
No kernel may reach another device: no remote copies, remote signals or barrier semaphores. Data moves between devices by JAX's collectives and lax.ppermute only.
A program may use at most 128 MiB of HBM per device.

v0:
```python
import math
import jax
import jax.numpy as jnp
from jax import lax
from jax.sharding import PartitionSpec as P


def side_by_side(arrays, axis, dim, along):
    widths = [math.prod(a.shape[along:]) for a in arrays]
    both = jnp.concatenate(
        [a.reshape(*a.shape[:along], w) for a, w in zip(arrays, widths)], axis=along
    )
    out = lax.all_gather(both, axis, axis=dim, tiled=True)
    parts = jnp.split(out, [sum(widths[:k]) for k in range(1, len(widths))], axis=along)
    return tuple((b.reshape(*out.shape[:along], *a.shape[along:]) for a, b in zip(arrays, parts)))


def from_everyone(x, axis):
    copies = jnp.broadcast_to(x, (lax.axis_size(axis), *x.shape))
    return lax.all_to_all(copies, axis, split_axis=0, concat_axis=0, tiled=True)


def of_everyone(x, axis):
    return from_everyone(x, axis).sum(axis=0)


def block_slots(prompt_block_count, request_adapter, adapter_bank_row, block_total):
    block_ids = jnp.arange(block_total, dtype=jnp.int32)
    block_ends = jnp.cumsum(prompt_block_count)
    request_of = jnp.sum((block_ends[None, :] <= block_ids[:, None]).astype(jnp.int32), axis=1)
    request_ids = jnp.arange(prompt_block_count.shape[0], dtype=jnp.int32)
    adapter_of = jnp.sum(
        jnp.where(request_of[:, None] == request_ids[None, :], request_adapter[None, :], 0), axis=1
    )
    adapter_rows = jnp.arange(adapter_bank_row.shape[0], dtype=jnp.int32)
    return jnp.sum(
        jnp.where(adapter_of[:, None] == adapter_rows[None, :], adapter_bank_row[None, :], 0),
        axis=1,
    )


def body(
    hidden,
    key_value_weight,
    adapter_down_weight,
    adapter_up_weight,
    prompt_block_count,
    request_adapter,
    adapter_bank_row,
):
    owners = lax.axis_size("aa")
    owner_index = lax.axis_index("aa")
    shard_count = lax.axis_size(("ba", "col"))
    local_blocks, block_len, feat_width = hidden.shape
    request_grouped, paired_rank, unused_item = adapter_down_weight.shape
    rank_half = paired_rank // 2
    column_span = adapter_up_weight.shape[2]
    bank_row_lookup = block_slots(
        prompt_block_count, request_adapter, adapter_bank_row, local_blocks * owners
    )
    my_slots = lax.dynamic_slice_in_dim(bank_row_lookup, owner_index * local_blocks, local_blocks)
    token_rows = hidden.reshape(local_blocks * block_len, feat_width)
    partial_sums = lax.dot_general(
        token_rows,
        lax.all_gather(key_value_weight, "aa", axis=0, tiled=True),
        (((1,), (1,)), ((), ())),
        preferred_element_type=jnp.float32,
    )
    down_weight_slice, up_weight_slice = side_by_side(
        (adapter_down_weight, adapter_up_weight), "aa", 0, 1
    )
    bank_rows = jnp.arange(down_weight_slice.shape[0], dtype=jnp.int32)
    onehot = (my_slots[:, None] == bank_rows[None, :]).astype(jnp.bfloat16)
    down_add = jnp.einsum(
        "cn,nrf->crf", onehot, down_weight_slice, preferred_element_type=jnp.float32
    )
    up_weight_extra = jnp.einsum(
        "cn,nrj->crj", onehot, up_weight_slice, preferred_element_type=jnp.float32
    )
    down_sel = down_add
    down_sel = down_sel.astype(jnp.bfloat16)
    base_output = lax.psum_scatter(partial_sums, ("ba", "col"), scatter_dimension=1, tiled=True)
    low_part = jnp.einsum("ctf,crf->ctr", hidden, down_sel, preferred_element_type=jnp.float32)
    low_rank = of_everyone(low_part, ("ba", "col"))
    first_col = lax.axis_index(("ba", "col")) * column_span
    active_rank = jnp.where(
        first_col < column_span * shard_count // 2,
        low_rank[:, :, :rank_half],
        low_rank[:, :, rank_half:],
    )
    adapter_output = jnp.einsum(
        "qvy,qyz->qvz", active_rank, up_weight_extra, precision=lax.Precision.HIGHEST
    )
    base_output = base_output.reshape(local_blocks, block_len, column_span)
    return (base_output + adapter_output).astype(jnp.bfloat16)


def solution(mesh):
    placed = (
        P(("groups", "aa"), None, ("ba", "col")),
        P("aa", ("ba", "col")),
        P(("groups", "aa"), None, ("ba", "col")),
        P(("groups", "aa"), None, ("ba", "col")),
        P("groups"),
        P("groups"),
        P("groups"),
    )
    return jax.shard_map(
        body,
        mesh=mesh,
        in_specs=placed,
        out_specs=P(("groups", "aa"), None, ("ba", "col")),
        check_vma=False,
    )
```

profile of v0, /device:TPU:33, one launch (start us, length us, event | category | flops | bytes accessed | tf_op | source)
XLA Modules:
  0.0 386.0 jit_solution(8711361571595567866)
XLA Ops:
  6.5 0.0 copy-start
  6.6 0.0 all-gather.4.cloned.1.call-start
  6.6 0.7 all-gather.4.cloned.1.call-update
  7.3 0.1 all-gather.6.cloned.1.call-start
  7.4 0.8 copy.38
  8.2 1.2 copy.37
  9.3 0.9 maximum_bitcast_fusion
  10.2 0.1 all-gather.6.cloned.1.call-update
  10.2 0.1 reduce-scatter.2.cloned.1.call-start
  10.3 145.4 %all-gather.4.cloned.1.call-done = bf16[2048,1024]{1,0:T(8,128)(2,1)} async-done(((bf16[64,1024]{1,0:T(8,128)(2,1)}), bf16[2048,1024]{1,0:T(8,128)(2,1)}) %all-gather.4.cloned.1.call-update) | async-done | bytes 4194320 | tf_op jit(solution)/shard_map/all_gather | solution.py:65
  155.7 0.0 copy-done
  155.8 0.0 copy-start.1
  155.8 0.0 copy-start.2
  155.8 0.0 copy-start.3
  155.8 6.7 %fusion.11 = f32[512,2048]{1,0:T(8,128)} fusion(bf16[512,1024]{1,0:T(8,128)(2,1)S(1)} %bitcast.22, bf16[2048,1024]{1,0:T(8,128)(2,1)} %all-gather.4.cloned.1.call-done), kind=kOutput, calls=%fused_computation.21 | convolution fusion | flops 2147483648 | bytes 9437184 | tf_op jit(solution)/shard_map/dot_general | solution.py:63
  162.4 0.1 reduce-scatter.2.cloned.1.call-update
  162.5 0.0 copy-done.1
  162.5 0.1 copy.28
  162.6 0.1 reduce-window.8
  162.7 0.1 reduce
  162.8 0.1 convert_reduce_fusion
  162.9 0.0 copy-done.2
  162.9 0.1 select_reduce_fusion.1
  163.0 0.0 copy-done.3
  163.0 0.2 select_reduce_fusion
  163.2 0.1 dynamic_slice.3
  163.3 140.5 %all-gather.6.cloned.1.call-done = bf16[32,4,36864]{2,1,0:T(4,128)(2,1)} async-done(((bf16[1,4,36864]{2,1,0:T(4,128)(2,1)}), bf16[32,4,36864]{2,1,0:T(4,128)(2,1)}) %all-gather.6.cloned.1.call-update) | async-done | bytes 9437200 | tf_op jit(solution)/shard_map/all_gather | solution.py:13
  303.8 13.3 %reshape.56 = bf16[128,36864]{1,0:T(8,128)(2,1)} reshape(bf16[32,4,36864]{2,1,0:T(4,128)(2,1)} %all-gather.6.cloned.1.call-done) | data formatting | bytes 18874368
  317.1 7.4 %split.8 = bf16[128,32768]{1,0:T(8,128)(2,1)} slice(bf16[128,36864]{1,0:T(8,128)(2,1)} %reshape.56), slice={[0:128], [0:32768]} | slice | bytes 16777216 | tf_op jit(solution)/shard_map/split | solution.py:14
  324.5 12.0 %copy.29 = bf16[128,32768]{0,1:T(8,128)(2,1)} copy(bf16[128,32768]{1,0:T(8,128)(2,1)} %split.8) | data formatting | bytes 16777216 | tf_op jit(solution)/shard_map/split | solution.py:14
  336.5 0.0 slice-start
  336.5 5.8 %convolution_convert_fusion = bf16[4,32,1024]{2,0,1:T(4,128)(2,1)S(1)} fusion(bf16[128,32,1024]{0,2,1:T(8,128)(2,1)} %bitcast.23, s32[4]{0:T(128)S(1)} %dynamic_slice.3), kind=kOutput, calls=%fused_computation.2 | convolution fusion | flops 33686016 | bytes 8650768 | tf_op jit(solution)/shard_map/cn,nrf->crf/dot_general | solution.py:74
  342.3 0.5 convolution_bitcast_fusion
  342.7 0.9 broadcast_in_dim.41
  343.6 22.9 %all-to-all-start = ((f32[8,4,128,32]{2,3,1,0:T(8,128)}), f32[8,4,128,32]{2,3,1,0:T(8,128)}, u32[]{:S(2)}, u32[]{:S(2)}) async-start(f32[8,4,128,32]{2,3,1,0:T(8,128)} %broadcast_in_dim.41), calls=%async_computation.1 | async-start | bytes 1048576 | tf_op jit(solution)/shard_map/all_to_all | solution.py:20
  366.5 0.0 slice-done
  366.5 0.7 copy.32
  367.2 0.4 fusion.6
  367.6 8.4 %all-to-all-done = f32[8,4,128,32]{2,3,1,0:T(8,128)} async-done(((f32[8,4,128,32]{2,3,1,0:T(8,128)}), f32[8,4,128,32]{2,3,1,0:T(8,128)}, u32[]{:S(2)}, u32[]{:S(2)}) %all-to-all-start) | async-done | bytes 524320 | tf_op jit(solution)/shard_map/all_to_all | solution.py:20
  376.0 1.1 reduce_sum.39
  377.1 0.0 reduce-scatter.2.cloned.1.call-done
  377.1 2.4 fusion
Async XLA Ops:
  6.5 149.2 %copy-start = (bf16[4,128,1024]{2,1,0:T(8,128)(2,1)S(1)}, bf16[4,128,1024]{2,1,0:T(8,128)(2,1)}, u32[]{:S(2)}) copy-start(bf16[4,128,1024]{2,1,0:T(8,128)(2,1)} %param.7) | copy-start | bytes 3145732
  6.6 149.2 %all-gather.4.cloned.1.call-start = ((), (), s32[]{:S(2)}) async-start(), calls=%async_computation.2 | async-start | bytes 4325376 | tf_op jit(solution)/shard_map/all_gather | solution.py:65
  7.3 296.5 %all-gather.6.cloned.1.call-start = ((), (), s32[]{:S(2)}) async-start(), calls=%async_computation.4 | async-start | bytes 9732096 | tf_op jit(solution)/shard_map/all_gather | solution.py:13
  10.2 366.8 %reduce-scatter.2.cloned.1.call-start = ((), (), s32[]{:S(2)}) async-start(), calls=%async_computation.3 | async-start | bytes 4718592 | tf_op jit(solution)/shard_map/reduce_scatter | solution.py:82
  155.8 6.7 %copy-start.1 = (s32[64]{0:T(128)S(1)}, s32[64]{0:T(128)}, u32[]{:S(2)}) copy-start(s32[64]{0:T(128)} %param.11) | copy-start | bytes 772
  155.8 7.2 %copy-start.2 = (s32[64]{0:T(128)S(1)}, s32[64]{0:T(128)}, u32[]{:S(2)}) copy-start(s32[64]{0:T(128)} %param.12) | copy-start | bytes 772
  155.8 7.3 %copy-start.3 = (s32[128]{0:T(128)S(1)}, s32[128]{0:T(128)}, u32[]{:S(2)}) copy-start(s32[128]{0:T(128)} %param.13) | copy-start | bytes 1540
  336.5 30.0 %slice-start = ((bf16[128,36864]{1,0:T(8,128)(2,1)}), bf16[128,4096]{1,0:T(8,128)(2,1)S(1)}, s32[]{:S(2)}) async-start(bf16[128,36864]{1,0:T(8,128)(2,1)} %reshape.56), calls=%async_computation.5 | async-start | bytes 2097152 | tf_op jit(solution)/shard_map/split | solution.py:14
  343.6 32.4 %all-to-all-start = ((f32[8,4,128,32]{2,3,1,0:T(8,128)}), f32[8,4,128,32]{2,3,1,0:T(8,128)}, u32[]{:S(2)}, u32[]{:S(2)}) async-start(f32[8,4,128,32]{2,3,1,0:T(8,128)} %broadcast_in_dim.41), calls=%async_computation.1 | async-start | bytes 1048576 | tf_op jit(solution)/shard_map/all_to_all | solution.py:20
Sparse Core Ops, SparseCore 0:
  9.4 146.2 all-gather.3
  157.8 145.9 all-gather.5
  306.7 62.0 reduce-scatter.1
where the time goes:
time: 387 us; the launch traced here: 386 us
  waiting for transfers between devices  295 us (76%)
  local copies, waits for them, and re-layouts  36.3 us (9%)
  starting transfers between devices  23 us (6%)
  matrix products  15.7 us (4%)
  between operations  13.2 us (3%)
    all_gather x1, waiting for transfers between devices, body(): lax.all_gather(key_value_weight, 'aa', axis=0, tiled=True)  145 us
    all_gather x1, waiting for transfers between devices, side_by_side(): out = lax.all_gather(both, axis, axis=dim, tiled=True)  141 us
    all_to_all x1, starting transfers between devices, from_everyone(): return lax.all_to_all(copies, axis, split_axis=0, concat_axis=0, tiled=True)  22.9 us
    split x5, local copies, waits for them, and re-layouts, side_by_side(): jnp.split(out, [sum(widths[:k]) for k in range(1, len(widths))], axis=along)  20.1 us
    unnamed x11, local copies, waits for them, and re-layouts  15.2 us
    all_to_all x1, waiting for transfers between devices, from_everyone(): return lax.all_to_all(copies, axis, split_axis=0, concat_axis=0, tiled=True)  8.39 us
  transfers between devices with their start and end apart: 4, of which 3 were waited for; matrix products, arithmetic and copies ran while one was open for 14% of the time, Pallas kernels for 0%

commit v1 on v0

--- a/solution.py
+++ b/solution.py
@@ -1,8 +1,20 @@
+import functools
 import math
 import jax
 import jax.numpy as jnp
 from jax import lax
 from jax.sharding import PartitionSpec as P
+
+
+def turns_wrap(v0, mesh_name, where_dim):
+    wide_n = lax.psum(1, mesh_name)
+    entries = list(map(lambda ii: wide_n if ii == where_dim else 1, range(v0.ndim)))
+    return lax.all_to_all(
+        jnp.tile(v0, entries), mesh_name, split_axis=where_dim, concat_axis=where_dim, tiled=True
+    )
+
+
+see_side_now = functools.partial(turns_wrap, mesh_name="aa", where_dim=0)
 
 
 def side_by_side(arrays, axis, dim, along):
@@ -62,7 +74,7 @@
     token_rows = hidden.reshape(local_blocks * block_len, feat_width)
     partial_sums = lax.dot_general(
         token_rows,
-        lax.all_gather(key_value_weight, "aa", axis=0, tiled=True),
+        see_side_now(key_value_weight),
         (((1,), (1,)), ((), ())),
         preferred_element_type=jnp.float32,
     )

time: 387 us -> 602 us (1.56)
  waiting for transfers between devices: 295 us -> 468 us
  starting transfers between devices: 23 us -> 61.4 us
    all_to_all x0 -> x1, waiting for transfers between devices: none -> 419 us  [turns_wrap(): lax.all_to_all(jnp.tile(v0, entries), mesh_name, split_axis=where_dim, co...]
    all_gather x1 -> x0, waiting for transfers between devices: 145 us -> none  [body(): lax.all_gather(key_value_weight, 'aa', axis=0, tiled=True)]
    all_gather x1, waiting for transfers between devices: 141 us -> 40.6 us  [side_by_side(): out = lax.all_gather(both, axis, axis=dim, tiled=True)]
    all_to_all x0 -> x1, starting transfers between devices: none -> 46.3 us  [turns_wrap(): lax.all_to_all(jnp.tile(v0, entries), mesh_name, split_axis=where_dim, co...]
    all_to_all x1, starting transfers between devices: 22.9 us -> 14.9 us  [from_everyone(): return lax.all_to_all(copies, axis, split_axis=0, concat_axis=0, tiled=True)]
    unnamed x11 -> x15, local copies, waits for them, and re-layouts: 15.2 us -> 13.5 us
  transfers between devices with their start and end apart: 4 -> 4, of which waited for: 3 -> 3; matrix products, arithmetic and copies ran while one was open for 14% -> 8% of each run, Pallas kernels for 0% -> 0%
where the time goes in v1:
time: 602 us; the launch traced here: 601 us
  waiting for transfers between devices  468 us (78%)
  starting transfers between devices  61.4 us (10%)
  local copies, waits for them, and re-layouts  38.1 us (6%)
  matrix products  15.7 us (3%)
  between operations  15 us (2%)
    all_to_all x1, waiting for transfers between devices, turns_wrap(): lax.all_to_all(jnp.tile(v0, entries), mesh_name, split_axis=where_dim, co...  419 us
    all_to_all x1, starting transfers between devices, turns_wrap(): lax.all_to_all(jnp.tile(v0, entries), mesh_name, split_axis=where_dim, co...  46.3 us
    all_gather x1, waiting for transfers between devices, side_by_side(): out = lax.all_gather(both, axis, axis=dim, tiled=True)  40.6 us
    split x5, local copies, waits for them, and re-layouts, side_by_side(): jnp.split(out, [sum(widths[:k]) for k in range(1, len(widths))], axis=along)  20.1 us
    all_to_all x1, starting transfers between devices, from_everyone(): return lax.all_to_all(copies, axis, split_axis=0, concat_axis=0, tiled=True)  14.9 us
    unnamed x15, local copies, waits for them, and re-layouts  13.5 us
  transfers between devices with their start and end apart: 4, of which 3 were waited for; matrix products, arithmetic and copies ran while one was open for 8% of the time, Pallas kernels for 0%

profile of v1, /device:TPU:33, one launch (start us, length us, event | category | flops | bytes accessed | tf_op | source)
XLA Modules:
  0.0 601.0 jit_solution(4712072963880281722)
XLA Ops:
  7.4 0.0 copy-start
  7.4 0.0 copy-start.2
  7.4 0.0 copy-start.1
  7.4 3.5 tile.2
  10.9 46.3 %all-to-all-start = ((bf16[32,64,1024]{2,1,0:T(8,128)(2,1)}), bf16[32,64,1024]{2,1,0:T(8,128)(2,1)}, u32[]{:S(2)}, u32[]{:S(2)}) async-start(bf16[32,64,1024]{2,1,0:T(8,128)(2,1)} %tile.2), calls=%async_computation | async-start | bytes 8388608 | tf_op jit(solution)/shard_map/all_to_all | solution.py:12
  57.2 0.1 all-gather.3.cloned.1.call-start
  57.3 0.0 copy-done.2
  57.3 0.0 copy-done.1
  57.3 0.2 copy.37
  57.5 0.9 maximum_bitcast_fusion
  58.4 0.1 all-gather.3.cloned.1.call-update
  58.5 0.1 reduce-scatter.2.cloned.1.call-start
  58.5 419.1 %all-to-all-done = bf16[32,64,1024]{2,1,0:T(8,128)(2,1)} async-done(((bf16[32,64,1024]{2,1,0:T(8,128)(2,1)}), bf16[32,64,1024]{2,1,0:T(8,128)(2,1)}, u32[]{:S(2)}, u32[]{:S(2)}) %all-to-all-start) | async-done | bytes 4194336 | tf_op jit(solution)/shard_map/all_to_all | solution.py:12
  477.6 0.0 copy-done
  477.6 0.0 copy-start.3
  477.6 0.0 copy-start.4
  477.6 0.0 copy-start.5
  477.6 6.7 %fusion.11 = f32[512,2048]{1,0:T(8,128)} fusion(bf16[512,1024]{1,0:T(8,128)(2,1)S(1)} %bitcast.23, bf16[2048,1024]{1,0:T(8,128)(2,1)} %bitcast.1), kind=kOutput, calls=%fused_computation.21 | convolution fusion | flops 2147483648 | bytes 9437184 | tf_op jit(solution)/shard_map/dot_general | solution.py:75
  484.3 0.1 reduce-scatter.2.cloned.1.call-update
  484.4 0.0 copy-done.3
  484.4 0.1 copy.28
  484.5 0.1 reduce-window.8
  484.6 0.1 reduce
  484.7 0.1 convert_reduce_fusion
  484.8 0.0 copy-done.4
  484.8 0.1 select_reduce_fusion.1
  484.9 0.0 copy-done.5
  484.9 0.2 select_reduce_fusion
  485.1 0.1 dynamic_slice.3
  485.2 40.6 %all-gather.3.cloned.1.call-done = bf16[32,4,36864]{2,1,0:T(4,128)(2,1)} async-done(((bf16[1,4,36864]{2,1,0:T(4,128)(2,1)}), bf16[32,4,36864]{2,1,0:T(4,128)(2,1)}) %all-gather.3.cloned.1.call-update) | async-done | bytes 9437200 | tf_op jit(solution)/shard_map/all_gather | solution.py:25
  525.7 13.3 %reshape.63 = bf16[128,36864]{1,0:T(8,128)(2,1)} reshape(bf16[32,4,36864]{2,1,0:T(4,128)(2,1)} %all-gather.3.cloned.1.call-done) | data formatting | bytes 18874368
  539.0 7.4 %split.8 = bf16[128,32768]{1,0:T(8,128)(2,1)} slice(bf16[128,36864]{1,0:T(8,128)(2,1)} %reshape.63), slice={[0:128], [0:32768]} | slice | bytes 16777216 | tf_op jit(solution)/shard_map/split | solution.py:26
  546.5 12.0 %copy.29 = bf16[128,32768]{0,1:T(8,128)(2,1)} copy(bf16[128,32768]{1,0:T(8,128)(2,1)} %split.8) | data formatting | bytes 16777216 | tf_op jit(solution)/shard_map/split | solution.py:26
  558.4 0.0 slice-start
  558.4 5.8 convolution_convert_fusion
  564.2 0.5 convolution_bitcast_fusion
  564.7 0.9 broadcast_in_dim.41
  565.6 14.9 %all-to-all-start.1 = ((f32[8,4,128,32]{2,3,1,0:T(8,128)}), f32[8,4,128,32]{2,3,1,0:T(8,128)}, u32[]{:S(2)}, u32[]{:S(2)}) async-start(f32[8,4,128,32]{2,3,1,0:T(8,128)} %broadcast_in_dim.41), calls=%async_computation.2 | async-start | bytes 1048576 | tf_op jit(solution)/shard_map/all_to_all | solution.py:32
  580.5 0.0 slice-done
  580.5 0.7 copy.32
  581.1 0.4 fusion.6
  581.5 8.5 %all-to-all-done.1 = f32[8,4,128,32]{2,3,1,0:T(8,128)} async-done(((f32[8,4,128,32]{2,3,1,0:T(8,128)}), f32[8,4,128,32]{2,3,1,0:T(8,128)}, u32[]{:S(2)}, u32[]{:S(2)}) %all-to-all-start.1) | async-done | bytes 524320 | tf_op jit(solution)/shard_map/all_to_all | solution.py:32
  590.0 1.1 reduce_sum.39
  591.1 0.0 reduce-scatter.2.cloned.1.call-done
  591.1 2.4 fusion
  (1 shorter events, 0.0 us)
Async XLA Ops:
  7.4 470.2 %copy-start = (bf16[4,128,1024]{2,1,0:T(8,128)(2,1)S(1)}, bf16[4,128,1024]{2,1,0:T(8,128)(2,1)}, u32[]{:S(2)}) copy-start(bf16[4,128,1024]{2,1,0:T(8,128)(2,1)} %param.7) | copy-start | bytes 3145732
  7.4 49.9 %copy-start.2 = (bf16[4,16,256]{2,1,0:T(8,128)(2,1)S(1)}, bf16[4,16,256]{2,1,0:T(8,128)(2,1)}, u32[]{:S(2)}) copy-start(bf16[4,16,256]{2,1,0:T(8,128)(2,1)} %param.10) | copy-start | bytes 98308
  7.4 49.9 %copy-start.1 = (bf16[4,32,1024]{2,1,0:T(8,128)(2,1)S(1)}, bf16[4,32,1024]{2,1,0:T(8,128)(2,1)}, u32[]{:S(2)}) copy-start(bf16[4,32,1024]{2,1,0:T(8,128)(2,1)} %param.9) | copy-start | bytes 786436
  10.9 466.7 %all-to-all-start = ((bf16[32,64,1024]{2,1,0:T(8,128)(2,1)}), bf16[32,64,1024]{2,1,0:T(8,128)(2,1)}, u32[]{:S(2)}, u32[]{:S(2)}) async-start(bf16[32,64,1024]{2,1,0:T(8,128)(2,1)} %tile.2), calls=%async_computation | async-start | bytes 8388608 | tf_op jit(solution)/shard_map/all_to_all | solution.py:12
  57.2 468.5 %all-gather.3.cloned.1.call-start = ((), (), s32[]{:S(2)}) async-start(), calls=%async_computation.4 | async-start | bytes 9732096 | tf_op jit(solution)/shard_map/all_gather | solution.py:25
  58.5 532.7 %reduce-scatter.2.cloned.1.call-start = ((), (), s32[]{:S(2)}) async-start(), calls=%async_computation.3 | async-start | bytes 4718592 | tf_op jit(solution)/shard_map/reduce_scatter | solution.py:94
  477.6 6.8 %copy-start.3 = (s32[64]{0:T(128)S(1)}, s32[64]{0:T(128)}, u32[]{:S(2)}) copy-start(s32[64]{0:T(128)} %param.11) | copy-start | bytes 772
  477.6 7.2 %copy-start.4 = (s32[64]{0:T(128)S(1)}, s32[64]{0:T(128)}, u32[]{:S(2)}) copy-start(s32[64]{0:T(128)} %param.12) | copy-start | bytes 772
  477.6 7.3 %copy-start.5 = (s32[128]{0:T(128)S(1)}, s32[128]{0:T(128)}, u32[]{:S(2)}) copy-start(s32[128]{0:T(128)} %param.13) | copy-start | bytes 1540
  558.4 22.0 %slice-start = ((bf16[128,36864]{1,0:T(8,128)(2,1)}), bf16[128,4096]{1,0:T(8,128)(2,1)S(1)}, s32[]{:S(2)}) async-start(bf16[128,36864]{1,0:T(8,128)(2,1)} %reshape.63), calls=%async_computation.5 | async-start | bytes 2097152 | tf_op jit(solution)/shard_map/split | solution.py:26
  565.6 24.5 %all-to-all-start.1 = ((f32[8,4,128,32]{2,3,1,0:T(8,128)}), f32[8,4,128,32]{2,3,1,0:T(8,128)}, u32[]{:S(2)}, u32[]{:S(2)}) async-start(f32[8,4,128,32]{2,3,1,0:T(8,128)} %broadcast_in_dim.41), calls=%async_computation.2 | async-start | bytes 1048576 | tf_op jit(solution)/shard_map/all_to_all | solution.py:32
Sparse Core Ops, SparseCore 0:
  60.1 465.5 all-gather.2
Sparse Core Ops, SparseCore 1:
  484.5 36.7 reduce-scatter.1
